TPU v7x, 32 devices: a whole 2x2x4 slice. The times are simulated.
32 devices in a mesh: dp: 4 (over y, x), expert: 4 (over z), tensor: 2 (over core).
Axes of the slice: x: 2, y: 2, z: 4, core: 2. Of those that a mesh axis runs over, the one named last changes fastest.
Arguments:
- tokens: bfloat16 [2048, 2048], P(('dp', 'expert'), 'tensor'), may hold values from -6 to 6
- norm_gain: bfloat16 [2048], replicated, may hold values from 0.25 to 1.75
- expert_ids: int32 [2048, 2], P(('dp', 'expert')), may hold values from 0 to 3, all different within a row; in each aligned block of 128 rows (0 to 127, 128 to 255, ...) at most 128 rows name the same one
- gate_codes: int32 [2048, 2], P(('dp', 'expert')), may hold values from 1 to 255
- gate_weights: bfloat16 [4, 7168, 2048], P('expert', ('dp', 'tensor')), may hold values from -0.125 to 0.125
- up_weights: bfloat16 [4, 7168, 2048], P('expert', ('dp', 'tensor')), may hold values from -0.125 to 0.125
- down_weights: bfloat16 [4, 7168, 2048], P('expert', ('dp', 'tensor')), may hold values from -0.0625 to 0.0625
- value_head: bfloat16 [2048, 128], replicated, may hold values from -0.125 to 0.125
- actions: int32 [2048], P(('dp', 'expert')), may hold values from 0 to 127
- rewards: int32 [2048], P(('dp', 'expert')), may hold values from -8 to 8
- trace_codes: int32 [2048], P(('dp', 'expert')), may hold values from 1 to 1024
Outputs:
- action_values: float32 [2048, 128], P(('dp', 'expert'))
- retrace_targets: float32 [2048], P(('dp', 'expert'))
Inputs may be any that keep to these rules, and one draw needn't show every extreme that they name: `expert_ids`: each row names 2 different experts; within the 128 rows of one index pair of dp and expert each expert is named by at most 128 rows, and in some of these blocks one expert by exactly 128.
All inputs are finite; a program needn't handle non-finite values.
Results may differ from a plain program's by a relative error of at most 0.005.
Values may be sent and summed in bfloat16 or wider, within the bound.
A program may use at most 256 MiB of HBM per device.

v0:
```python
import jax
import jax.numpy as jnp
from jax import lax
from jax.sharding import PartitionSpec as P

TOP = 2
STEPS = 128


DISCOUNT = 0.99
EPSILON = 1e-05


def expert_rows(row_block, gate_matrix, lift_matrix, down_matrix):
    gate_value = lax.dot_general(
        row_block, gate_matrix, (((1,), (1,)), ((), ())), preferred_element_type=jnp.float32
    )
    lift_value = lax.dot_general(
        row_block, lift_matrix, (((1,), (1,)), ((), ())), preferred_element_type=jnp.float32
    )
    hidden = (jax.nn.silu(gate_value) * lift_value).astype(jnp.bfloat16)
    return jnp.dot(hidden, down_matrix, preferred_element_type=jnp.float32)


def retrace(action_values, actions, rewards, trace_codes):
    greedy = jnp.max(action_values, axis=1)
    picked = (
        actions[:, None] == jnp.arange(action_values.shape[1], dtype=jnp.int32)[None, :]
    ).astype(jnp.float32)
    taken = jnp.sum(action_values * picked, axis=1)
    trace = trace_codes.astype(jnp.float32) / 1024.0
    reward = rewards.astype(jnp.float32) * 0.25
    greedy = greedy.reshape(-1, STEPS)
    taken = taken.reshape(-1, STEPS)
    trace = trace.reshape(-1, STEPS)
    reward = reward.reshape(-1, STEPS)
    padding = jnp.zeros_like(greedy[:, :1])
    greedy_next = jnp.concatenate([greedy[:, 1:], padding], axis=1)
    taken_next = jnp.concatenate([taken[:, 1:], padding], axis=1)
    trace_next = jnp.concatenate([trace[:, 1:], padding], axis=1)
    driver = reward + DISCOUNT * (greedy_next - trace_next * taken_next)
    log_sums = jnp.cumsum(jnp.log(DISCOUNT * trace), axis=1)
    spans = log_sums[:, None, :] - log_sums[:, :, None]
    upper_mask = (
        jnp.arange(STEPS, dtype=jnp.int32)[None, :] >= jnp.arange(STEPS, dtype=jnp.int32)[:, None]
    )
    weight = jnp.where(upper_mask[None, :, :], jnp.exp(jnp.minimum(spans, 0.0)), 0.0)
    target = jnp.einsum("nts,ns->nt", weight, driver, precision=lax.Precision.HIGHEST)
    return target.reshape(-1)


def per_device(
    tokens,
    norm_gain,
    expert_ids,
    gate_codes,
    gate_weights,
    up_weights,
    down_weights,
    value_head,
    actions,
    rewards,
    trace_codes,
):
    groups = lax.axis_size("expert")
    tok_rows = tokens.shape[0]
    capacity = 2 * tok_rows * TOP // groups
    head_wide = value_head.astype(jnp.float32)
    flat_ids = expert_ids.reshape(-1)
    marked = (flat_ids[:, None] == jnp.arange(groups, dtype=jnp.int32)[None, :]).astype(jnp.int32)
    places = jnp.sum((jnp.cumsum(marked, axis=0) - 1) * marked, axis=1)
    slot_of = (flat_ids * capacity + places).reshape(tok_rows, TOP)
    slot_range = jnp.arange(groups * capacity, dtype=jnp.int32)
    matches = slot_of[None, :, :] == slot_range[:, None, None]
    dispatch_map = jnp.any(matches, axis=2).astype(jnp.bfloat16)
    outgoing = jnp.dot(dispatch_map, tokens, preferred_element_type=jnp.float32).astype(
        jnp.bfloat16
    )
    outgoing = outgoing.reshape(groups, capacity, tokens.shape[1])
    arrived = lax.all_to_all(outgoing, "expert", split_axis=0, concat_axis=0, tiled=True)
    arrived = lax.all_gather(arrived, "tensor", axis=2, tiled=True)
    row_count = groups * capacity
    row_block = arrived.reshape(row_count, arrived.shape[2])
    widened = row_block.astype(jnp.float32)
    scaling = lax.rsqrt(jnp.mean(widened * widened, axis=1, keepdims=True) + EPSILON)
    normed = (widened * scaling * norm_gain.astype(jnp.float32)[None, :]).astype(jnp.bfloat16)
    gathered = lax.all_gather(normed, "dp", axis=0, tiled=True)
    payload = lax.psum_scatter(
        expert_rows(gathered, gate_weights[0], up_weights[0], down_weights[0]),
        "dp",
        scatter_dimension=0,
        tiled=True,
    )
    returned = lax.all_to_all(
        payload.reshape(groups, capacity, payload.shape[1]),
        "expert",
        split_axis=0,
        concat_axis=0,
        tiled=True,
    )
    returned = returned.reshape(row_count, payload.shape[1])
    codes = gate_codes.astype(jnp.float32)
    gate_share = codes / jnp.sum(codes, axis=1, keepdims=True)
    combine_map = jnp.sum(jnp.where(matches, gate_share[None, :, :], 0.0), axis=2)
    blended = lax.dot_general(
        combine_map,
        returned,
        (((0,), (0,)), ((), ())),
        precision=lax.Precision.HIGHEST,
        preferred_element_type=jnp.float32,
    )
    partial_values = jnp.dot(
        blended, head_wide, precision=lax.Precision.HIGHEST, preferred_element_type=jnp.float32
    )
    action_values = lax.psum(partial_values, "tensor")
    retrace_targets = retrace(action_values, actions, rewards, trace_codes)
    return (action_values, retrace_targets)


def solution(mesh):
    in_specs = (
        P(("dp", "expert"), "tensor"),
        P(),
        P(("dp", "expert"), None),
        P(("dp", "expert"), None),
        P("expert", ("dp", "tensor"), None),
        P("expert", ("dp", "tensor"), None),
        P("expert", ("dp", "tensor"), None),
        P(),
        P(("dp", "expert")),
        P(("dp", "expert")),
        P(("dp", "expert")),
    )
    out_specs = (P(("dp", "expert"), None), P(("dp", "expert")))
    return jax.shard_map(
        per_device, mesh=mesh, in_specs=in_specs, out_specs=out_specs, check_vma=False
    )
```

profile of v0, /device:TPU:0, one launch (start us, length us, event | category | flops | bytes accessed | tf_op | source)
XLA Modules:
  0.0 473.5 jit_solution(6893080322555966808)
XLA Ops:
  7.2 0.0 copy-start
  7.2 0.0 all-gather.3.cloned.1.call-start
  7.2 0.8 copy.34
  8.1 0.1 eq.53
  8.2 0.1 eq.49
  8.4 1.2 reduce-window.14
  9.6 0.1 slice.20
  9.7 0.1 copy.36
  9.8 0.1 copy.37
  9.9 0.1 add_bitcast_fusion
  10.0 0.1 reduce_sum.48
  10.2 0.1 copy.38
  10.2 0.7 multiply_add_fusion
  10.9 0.1 fusion.9
  11.0 1.4 convolution_convert_fusion
  12.4 32.0 %all_to_all.10 = bf16[4,128,1024]{2,1,0:T(8,128)(2,1)} all-to-all(bf16[4,128,1024]{2,1,0:T(8,128)(2,1)S(1)} %bitcast.62), channel_id=1, replica_groups=mesh['dp'=4,'expert'=4,'tensor'=2] {'expert'}, dimensions={0} | all-to-all | bytes 2097152 | tf_op jit(solution)/shard_map/all_to_all | solution.py:80
  44.3 0.0 all-gather.3.cloned.1.call-update
  44.4 0.0 all-gather.5.cloned.1.call-start
  44.4 0.0 copy-done.1
  44.4 9.8 %all-gather.3.cloned.1.call-done = bf16[4,128,2048]{2,1,0:T(8,128)(2,1)} async-done(((bf16[4,128,1024]{2,1,0:T(8,128)(2,1)}), bf16[4,128,2048]{2,1,0:T(8,128)(2,1)}) %all-gather.3.cloned.1.call-update) | async-done | bytes 2097168 | tf_op jit(solution)/shard_map/all_gather | solution.py:81
  54.2 2.1 multiply_reduce_fusion
  56.3 3.4 fusion.1
  59.7 0.0 all-gather.5.cloned.1.call-update
  59.7 0.2 reduce-scatter.2.cloned.1.call-start
  60.0 88.6 %all-gather.5.cloned.1.call-done = bf16[2048,2048]{1,0:T(8,128)(2,1)} async-done(((bf16[512,2048]{1,0:T(8,128)(2,1)}), bf16[2048,2048]{1,0:T(8,128)(2,1)}) %all-gather.5.cloned.1.call-update) | async-done | bytes 8388624 | tf_op jit(solution)/shard_map/all_gather | solution.py:87
  148.6 14.2 %fusion.6 = f32[2048,896]{1,0:T(8,128)} fusion(bf16[2048,2048]{1,0:T(8,128)(2,1)} %all-gather.5.cloned.1.call-done, bf16[1,896,2048]{2,1,0:T(8,128)(2,1)} %param.15), kind=kOutput, calls=%fused_computation.8 | convolution fusion | flops 7516192768 | bytes 19398656 | tf_op jit(solution)/shard_map/dot_general | solution.py:15
  162.8 26.7 %fusion.2 = f32[2048,2048]{1,0:T(8,128)} fusion(f32[2048,896]{1,0:T(8,128)} %fusion.6, bf16[2048,2048]{1,0:T(8,128)(2,1)} %all-gather.5.cloned.1.call-done, bf16[1,896,2048]{2,1,0:T(8,128)(2,1)} %param.17, bf16[1,896,2048]{2,1,0:T(8,128)(2,1)} %param.16), kind=kOutput, calls=%fused_computation.5 | convolution fusion | flops 15043395584 | bytes 39845888 | tf_op jit(solution)/shard_map/dot_general | solution.py:22
  189.5 0.0 reduce-scatter.2.cloned.1.call-update
  189.5 153.9 %reduce-scatter.2.cloned.1.call-done = f32[512,2048]{1,0:T(8,128)} async-done(((f32[2048,2048]{1,0:T(8,128)}), f32[512,2048]{1,0:T(8,128)}) %reduce-scatter.2.cloned.1.call-update) | async-done | bytes 4194320 | tf_op jit(solution)/shard_map/reduce_scatter | solution.py:88
  343.4 5.0 %all-to-all-start.1 = ((f32[4,128,2048]{2,1,0:T(8,128)}), f32[4,128,2048]{2,1,0:T(8,128)}, u32[]{:S(2)}, u32[]{:S(2)}) async-start(f32[4,128,2048]{2,1,0:T(8,128)} %bitcast.61), calls=%async_computation.2 | async-start | bytes 8388608 | tf_op jit(solution)/shard_map/all_to_all | solution.py:94
  348.4 0.0 copy-start.3
  348.4 0.0 copy-start.5
  348.4 0.3 all-reduce.2.cloned.1.call-start
  348.7 0.1 select_reduce_fusion
  348.8 0.0 copy-done.4
  348.8 92.9 %all-to-all-done.1 = f32[4,128,2048]{2,1,0:T(8,128)} async-done(((f32[4,128,2048]{2,1,0:T(8,128)}), f32[4,128,2048]{2,1,0:T(8,128)}, u32[]{:S(2)}, u32[]{:S(2)}) %all-to-all-start.1) | async-done | bytes 4194336 | tf_op jit(solution)/shard_map/all_to_all | solution.py:94
  441.7 4.6 fusion.34
  446.3 1.3 fusion.35
  447.5 0.0 all-reduce.2.cloned.1.call-update
  447.6 0.1 slice_bitcast_fusion.1
  447.6 0.1 copy.39
  447.8 0.2 reduce-window.19
  447.9 0.1 reduce.1
  448.0 15.5 %all-reduce.2.cloned.1.call-done = f32[128,128]{1,0:T(8,128)} async-done(((f32[128,128]{1,0:T(8,128)}), f32[128,128]{1,0:T(8,128)}) %all-reduce.2.cloned.1.call-update) | async-done | bytes 65552 | tf_op jit(solution)/shard_map/psum | solution.py:115
  463.6 1.0 select_reduce_fusion.1
  464.6 0.1 slice_bitcast_fusion
  464.6 0.8 convolution_bitcast_fusion
  465.5 1.5 copy.43
  (16 shorter events, 0.1 us)
Async XLA Ops:
  7.2 439.1 %copy-start = (bf16[2048,128]{1,0:T(8,128)(2,1)S(1)}, bf16[2048,128]{1,0:T(8,128)(2,1)}, u32[]{:S(2)}) copy-start(bf16[2048,128]{1,0:T(8,128)(2,1)} %param.18) | copy-start | bytes 1572868
  7.2 37.2 %copy-start.1 = (bf16[2048]{0:T(1024)(128)(2,1)S(1)}, bf16[2048]{0:T(1024)(128)(2,1)}, u32[]{:S(2)}) copy-start(bf16[2048]{0:T(1024)(128)(2,1)} %param.12) | copy-start | bytes 12292
  7.2 47.0 %all-gather.3.cloned.1.call-start = ((), (), s32[]{:S(2)}) async-start(), calls=%async_computation.3 | async-start | bytes 3145728 | tf_op jit(solution)/shard_map/all_gather | solution.py:81
  44.4 104.2 %all-gather.5.cloned.1.call-start = ((), (), s32[]{:S(2)}) async-start(), calls=%async_computation.4 | async-start | bytes 10485760 | tf_op jit(solution)/shard_map/all_gather | solution.py:87
  59.7 283.6 %reduce-scatter.2.cloned.1.call-start = ((), (), s32[]{:S(2)}) async-start(), calls=%async_computation.5 | async-start | bytes 20971520 | tf_op jit(solution)/shard_map/reduce_scatter | solution.py:88
  343.4 5.3 %copy-start.2 = (s32[128,2]{0,1:T(2,128)S(1)}, s32[128,2]{0,1:T(2,128)}, u32[]{:S(2)}) copy-start(s32[128,2]{0,1:T(2,128)} %param.14) | copy-start | bytes 3076
  343.4 5.4 %copy-start.4 = (s32[128]{0:T(128)S(1)}, s32[128]{0:T(128)}, u32[]{:S(2)}) copy-start(s32[128]{0:T(128)} %param.21) | copy-start | bytes 1540
  343.4 98.3 %all-to-all-start.1 = ((f32[4,128,2048]{2,1,0:T(8,128)}), f32[4,128,2048]{2,1,0:T(8,128)}, u32[]{:S(2)}, u32[]{:S(2)}) async-start(f32[4,128,2048]{2,1,0:T(8,128)} %bitcast.61), calls=%async_computation.2 | async-start | bytes 8388608 | tf_op jit(solution)/shard_map/all_to_all | solution.py:94
  348.4 115.2 %copy-start.3 = (s32[128]{0:T(128)S(1)}, s32[128]{0:T(128)}, u32[]{:S(2)}) copy-start(s32[128]{0:T(128)} %param.19) | copy-start | bytes 1540
  348.4 116.2 %copy-start.5 = (s32[128]{0:T(128)S(1)}, s32[128]{0:T(128)}, u32[]{:S(2)}) copy-start(s32[128]{0:T(128)} %param.20) | copy-start | bytes 1540
  348.4 115.1 %all-reduce.2.cloned.1.call-start = ((), (), s32[]{:S(2)}) async-start(), calls=%async_computation.6 | async-start | bytes 131072 | tf_op jit(solution)/shard_map/psum | solution.py:115
Sparse Core Ops, SparseCore 0:
  44.5 9.6 all-gather.2
  59.9 88.6 all-gather.4
  189.6 153.7 reduce-scatter.1
  447.7 15.8 all-reduce.1
where the time goes:
time: 474 us; the launch traced here: 473 us
  waiting for transfers between devices  361 us (76%)
  matrix products  48.9 us (10%)
  blocking collectives  32 us (7%)
  between operations  13.9 us (3%)
  other arithmetic  9.03 us (2%)
  starting transfers between devices  5.55 us (1%)
    reduce_scatter x1, waiting for transfers between devices, per_device(): lax.psum_scatter(expert_rows(gathered, gate_weights[0], up_weights[0], do...  154 us
    all_to_all x1, waiting for transfers between devices, per_device(): lax.all_to_all(payload.reshape(groups, capacity, payload.shape[1]), 'expe...  92.9 us
    all_gather x1, waiting for transfers between devices, per_device(): gathered = lax.all_gather(normed, 'dp', axis=0, tiled=True)  88.6 us
    all_to_all x1, blocking collectives, per_device(): lax.all_to_all(outgoing, 'expert', split_axis=0, concat_axis=0, tiled=True)  32 us
    dot_general x1, matrix products, expert_rows(): return jnp.dot(hidden, down_matrix, preferred_element_type=jnp.float32)  26.7 us
    psum x1, waiting for transfers between devices, per_device(): action_values = lax.psum(partial_values, 'tensor')  15.5 us
    dot_general x1, matrix products, expert_rows(): lax.dot_general(row_block, gate_matrix, (((1,), (1,)), ((), ())), preferr...  14.2 us
    all_gather x1, waiting for transfers between devices, per_device(): arrived = lax.all_gather(arrived, 'tensor', axis=2, tiled=True)  9.76 us
  transfers between devices with their start and end apart: 5, of which 5 were waited for; matrix products, arithmetic and copies ran while one was open for 0% of the time, Pallas kernels for 0%

commit v1 on v0

v1 whole, which is shorter than its diff:
```python
import jax
import jax.numpy as jnp
from jax import lax
from jax.experimental import pallas as pl
from jax.experimental.pallas import tpu as pltpu
from jax.sharding import PartitionSpec as P

TOP = 2
STEPS = 128


DISCOUNT = 0.99
EPSILON = 1e-05


def expert_rows(row_block, gate_matrix, lift_matrix, down_matrix):
    gate_value = lax.dot_general(
        row_block, gate_matrix, (((1,), (1,)), ((), ())), preferred_element_type=jnp.float32
    )
    lift_value = lax.dot_general(
        row_block, lift_matrix, (((1,), (1,)), ((), ())), preferred_element_type=jnp.float32
    )
    hidden = (jax.nn.silu(gate_value) * lift_value).astype(jnp.bfloat16)
    return jnp.dot(hidden, down_matrix, preferred_element_type=jnp.float32)


def retrace(action_values, actions, rewards, trace_codes):
    greedy = jnp.max(action_values, axis=1)
    picked = (
        actions[:, None] == jnp.arange(action_values.shape[1], dtype=jnp.int32)[None, :]
    ).astype(jnp.float32)
    taken = jnp.sum(action_values * picked, axis=1)
    trace = trace_codes.astype(jnp.float32) / 1024.0
    reward = rewards.astype(jnp.float32) * 0.25
    greedy = greedy.reshape(-1, STEPS)
    taken = taken.reshape(-1, STEPS)
    trace = trace.reshape(-1, STEPS)
    reward = reward.reshape(-1, STEPS)
    padding = jnp.zeros_like(greedy[:, :1])
    greedy_next = jnp.concatenate([greedy[:, 1:], padding], axis=1)
    taken_next = jnp.concatenate([taken[:, 1:], padding], axis=1)
    trace_next = jnp.concatenate([trace[:, 1:], padding], axis=1)
    driver = reward + DISCOUNT * (greedy_next - trace_next * taken_next)
    log_sums = jnp.cumsum(jnp.log(DISCOUNT * trace), axis=1)
    spans = log_sums[:, None, :] - log_sums[:, :, None]
    upper_mask = (
        jnp.arange(STEPS, dtype=jnp.int32)[None, :] >= jnp.arange(STEPS, dtype=jnp.int32)[:, None]
    )
    weight = jnp.where(upper_mask[None, :, :], jnp.exp(jnp.minimum(spans, 0.0)), 0.0)
    target = jnp.einsum("nts,ns->nt", weight, driver, precision=lax.Precision.HIGHEST)
    return target.reshape(-1)


def per_device_plain(
    tokens,
    norm_gain,
    expert_ids,
    gate_codes,
    gate_weights,
    up_weights,
    down_weights,
    value_head,
    actions,
    rewards,
    trace_codes,
):
    mesh_rows = ("dp", "expert")
    expert = lax.axis_index("expert")
    codes = gate_codes.astype(jnp.float32)
    gate_share = codes / jnp.sum(codes, axis=1, keepdims=True)
    experts = jnp.arange(lax.axis_size("expert"), dtype=jnp.int32)
    share = jnp.sum(
        jnp.where(expert_ids[:, :, None] == experts[None, None, :], gate_share[:, :, None], 0.0),
        axis=1,
    )
    every_share = lax.all_gather(share, mesh_rows, axis=0, tiled=True)
    own_share = lax.dynamic_slice_in_dim(every_share, expert, 1, axis=1)
    full = lax.all_gather(tokens, "tensor", axis=1, tiled=True)
    widened = full.astype(jnp.float32)
    scaling = lax.rsqrt(jnp.mean(widened * widened, axis=1, keepdims=True) + EPSILON)
    normed = (widened * scaling * norm_gain.astype(jnp.float32)[None, :]).astype(jnp.bfloat16)
    gathered = lax.all_gather(normed, mesh_rows, axis=0, tiled=True)
    scored = jnp.dot(down_weights[0], value_head, preferred_element_type=jnp.float32)
    high = scored.astype(jnp.bfloat16)
    low = (scored - high.astype(jnp.float32)).astype(jnp.bfloat16)
    both = jnp.concatenate([high, low], axis=1)
    wide = expert_rows(gathered, gate_weights[0], up_weights[0], both)
    actions_count = value_head.shape[1]
    partial_values = (wide[:, :actions_count] + wide[:, actions_count:]) * own_share
    partial_values = lax.psum_scatter(partial_values, mesh_rows, scatter_dimension=0, tiled=True)
    action_values = lax.psum(partial_values, "tensor")
    retrace_targets = retrace(action_values, actions, rewards, trace_codes)
    return (action_values, retrace_targets)


RING = 4
MESH = pl.DeviceIdType.MESH
TILE = 128
FIRST = ((0, 0), (1, 0), (3, 0), (0, 1), (0, 3))
SECOND = ((1, 1), (1, 3), (3, 1), (3, 3))
THIRD = ((2, 0), (0, 2), (2, 1), (1, 2))
FOURTH = ((2, 3), (3, 2), (2, 2))
GROUPS = (FIRST, SECOND, THIRD, FOURTH)


def gray(place):
    return place + (place // 2) * (1 - 2 * (place % 2))


def critic_kernel(
    tokens_ref,
    gain_ref,
    ids_ref,
    codes_ref,
    gate_ref,
    up_ref,
    down_ref,
    head_ref,
    actions_ref,
    rewards_ref,
    trace_ref,
    values_ref,
    targets_ref,
    raw,
    near,
    far,
    gate_buf,
    up_buf,
    down_buf,
    scored_buf,
    hidden_buf,
    sent,
    landed,
    share_buf,
    halves,
    load_sems,
    pair_send,
    pair_recv,
    ring_send,
    ring_recv,
    swap_send,
    swap_recv,
    back_send,
    back_recv,
):
    dp = lax.axis_index("dp")
    z = lax.axis_index("expert")
    core = lax.axis_index("tensor")
    other = 1 - core
    p = gray(dp)
    rows = tokens_ref.shape[0]
    half_rows = rows // 2
    part = near.shape[-1]
    wide = tokens_ref.shape[1]
    hidden_units = gate_ref.shape[1]
    actions_count = head_ref.shape[1]

    def device(step_p, step_z, which):
        return (gray((p + step_p) % RING), (z + step_z) % RING, which)

    load_token = pltpu.make_async_copy(tokens_ref, raw.at[core], load_sems.at[0])
    load_down = pltpu.make_async_copy(down_ref.at[0], down_buf, load_sems.at[1])
    load_gate = pltpu.make_async_copy(gate_ref.at[0], gate_buf, load_sems.at[2])
    load_up = pltpu.make_async_copy(up_ref.at[0], up_buf, load_sems.at[3])
    load_token.start()
    load_down.start()
    load_gate.start()
    load_up.start()

    barrier = pltpu.get_barrier_semaphore()
    for step_p in range(RING):
        for step_z in range(RING):
            for which in range(2):
                if (step_p, step_z, which) != (0, 0, 0):
                    pl.semaphore_signal(
                        barrier,
                        inc=1,
                        device_id=device(step_p, step_z, (core + which) % 2),
                        device_id_type=MESH,
                    )
    pl.semaphore_wait(barrier, 2 * RING * RING - 1)

    sends = []

    def send(source, target, send_sem, recv_sem, to):
        copy = pltpu.make_async_remote_copy(
            src_ref=source,
            dst_ref=target,
            send_sem=send_sem,
            recv_sem=recv_sem,
            device_id=to,
            device_id_type=MESH,
        )
        copy.start()
        sends.append(copy)

    def await_in(target, recv_sem):
        pltpu.make_async_remote_copy(
            src_ref=target,
            dst_ref=target,
            send_sem=recv_sem,
            recv_sem=recv_sem,
            device_id=device(0, 0, other),
            device_id_type=MESH,
        ).wait_recv()

    load_token.wait()
    send(raw.at[core], raw.at[core], pair_send.at[0], pair_recv.at[0], device(0, 0, other))
    first_axis = lax.broadcasted_iota(jnp.int32, (rows, rows), 0)
    second_axis = lax.broadcasted_iota(jnp.int32, (rows, rows), 1)
    same = first_axis == second_axis

    def column(row):
        return jnp.sum(jnp.where(same, row, 0.0), axis=1, keepdims=True)

    def row_of(col):
        return jnp.sum(jnp.where(same, col, 0.0), axis=0, keepdims=True)

    codes = codes_ref[...].astype(jnp.float32)
    gate_share = codes / jnp.sum(codes, axis=0, keepdims=True)
    ids = ids_ref[...]
    for expert in range(RING):
        share = jnp.sum(jnp.where(ids == expert, gate_share, 0.0), axis=0, keepdims=True)
        share_buf[expert] = jnp.broadcast_to(column(share), (rows, actions_count))

    await_in(raw.at[other], pair_recv.at[0])
    left = raw[0].astype(jnp.float32)
    right = raw[1].astype(jnp.float32)
    total = jnp.sum(left * left, axis=1, keepdims=True) + jnp.sum(
        right * right, axis=1, keepdims=True
    )
    scaling = lax.rsqrt(total / (2 * wide) + EPSILON)
    gain = gain_ref[...].astype(jnp.float32)
    for number, widened in enumerate((left, right)):
        normed = (widened * scaling * gain[:, number * wide : (number + 1) * wide]).astype(
            jnp.bfloat16
        )
        near[number, z, p] = normed[:, :part]
        far[number, p, z] = normed[:, part:]

    def block(kind, which, step_f, step_g):
        if kind == 0:
            return near.at[which, (z + step_g) % RING, (p + step_f) % RING]
        return far.at[which, (p + step_g) % RING, (z + step_f) % RING]

    def peer(kind, step_f, step_g):
        if kind == 0:
            return device(step_f, step_g, core)
        return device(step_g, step_f, core)

    def number_of(step_f, step_g):
        return step_g * RING + step_f

    half = (pl.ds(0, half_rows), pl.ds(half_rows, half_rows))

    def relay(kind, step_f, step_g, by_f, by_g, slot=None, cut=None):
        source = block(kind, core, step_f, step_g)
        seen = number_of((step_f - by_f) % RING, (step_g - by_g) % RING)
        if cut is not None:
            source = source.at[half[cut]]
            seen = RING * RING if cut == 1 else seen
        send(
            source,
            source,
            ring_send.at[kind, seen],
            ring_recv.at[kind, seen],
            peer(kind, by_f, by_g),
        )

    def arrive(kind, step_f, step_g):
        here = block(kind, core, step_f, step_g)
        seen = number_of(step_f, step_g)
        if (step_f, step_g) == (2, 0):
            await_in(here.at[half[0]], ring_recv.at[kind, seen])
            await_in(here.at[half[1]], ring_recv.at[kind, RING * RING])
        else:
            await_in(here, ring_recv.at[kind, seen])

    def swap(kind, step_f, step_g):
        here = block(kind, core, step_f, step_g)
        seen = number_of(step_f, step_g)
        send(
            here,
            here,
            swap_send.at[kind, seen],
            swap_recv.at[kind, seen],
            device(0, 0, other),
        )

    def swapped(kind, step_f, step_g):
        await_in(
            block(kind, other, step_f, step_g), swap_recv.at[kind, number_of(step_f, step_g)]
        )

    for kind in range(2):
        relay(kind, 0, 0, 1, 0)
        relay(kind, 0, 0, 3, 0)
    for kind in range(2):
        relay(kind, 0, 0, 0, 1)
        relay(kind, 0, 0, 0, 3)

    load_down.wait()
    scored = jnp.dot(down_buf[...], head_ref[...], preferred_element_type=jnp.float32)
    high = scored.astype(jnp.bfloat16)
    scored_buf[:, :actions_count] = high
    scored_buf[:, actions_count:] = (scored - high.astype(jnp.float32)).astype(jnp.bfloat16)

    for kind in range(2):
        for step_f in (1, 3):
            arrive(kind, step_f, 0)
            relay(kind, step_f, 0, (4 - step_f) % RING, 0, cut=0 if step_f == 3 else 1)
    for kind in range(2):
        for step_f in (1, 3):
            relay(kind, step_f, 0, 0, 1)
            relay(kind, step_f, 0, 0, 3)
            swap(kind, step_f, 0)
    for kind in range(2):
        arrive(kind, 2, 0)
        relay(kind, 2, 0, 0, 1)
        relay(kind, 2, 0, 0, 3)
        swap(kind, 2, 0)

    rising = (0, 1)

    def take(kind, step_f):
        for step_g in (1, 3):
            arrive(kind, step_f, step_g)
            if (step_g == 3) == (step_f in rising):
                relay(kind, step_f, step_g, 0, (4 - step_g) % RING)
            swap(kind, step_f, step_g)

    def kinds(step_p, step_z):
        return ((0, step_p, step_z), (1, step_z, step_p))

    def compute(group, base):
        for step_p, step_z in group:
            if (step_p, step_z) != (0, 0):
                for kind, step_f, step_g in kinds(step_p, step_z):
                    swapped(kind, step_f, step_g)
        lhs_rows = len(group) * rows

        def tile(index, carry):
            at = pl.ds(pl.multiple_of(index * TILE, TILE), TILE)
            weights = jnp.concatenate([gate_buf[at, :], up_buf[at, :]], axis=0)
            block_rows = []
            for step_p, step_z in group:
                zz, pp = (z + step_z) % RING, (p + step_p) % RING
                block_rows.append(
                    jnp.concatenate(
                        [near[0, zz, pp], far[0, pp, zz], near[1, zz, pp], far[1, pp, zz]],
                        axis=1,
                    )
                )
            lhs = jnp.concatenate(block_rows, axis=0)
            both = lax.dot_general(
                lhs, weights, (((1,), (1,)), ((), ())), preferred_element_type=jnp.float32
            )
            hidden = (jax.nn.silu(both[:, :TILE]) * both[:, TILE:]).astype(jnp.bfloat16)
            hidden_buf[:lhs_rows, at] = hidden
            return carry

        lax.fori_loop(0, hidden_units // TILE, tile, 0)
        result = jnp.dot(
            hidden_buf[:lhs_rows, :], scored_buf[...], preferred_element_type=jnp.float32
        )
        result = (result[:, :actions_count] + result[:, actions_count:]).astype(jnp.bfloat16)
        for place, (step_p, step_z) in enumerate(group):
            slot = base + place
            sent[slot] = result[place * rows : (place + 1) * rows]
            source = number_of((-step_p) % RING, (-step_z) % RING)
            own = (step_p, step_z) == (0, 0)
            if own:
                landed[z, p, core] = sent[
                    slot, pl.ds(pl.multiple_of(core * half_rows, half_rows), half_rows), :
                ]
                targets = ((other, 1),)
            else:
                targets = ((0, core % 2), (1, (core + 1) % 2))
            for which, relative in targets:
                cut = pl.ds(pl.multiple_of(which * half_rows, half_rows), half_rows)
                send(
                    sent.at[slot, cut],
                    landed.at[z, p, core],
                    back_send.at[2 * slot + which],
                    back_recv.at[2 * source + relative],
                    device(step_p, step_z, which),
                )

    for kind in range(2):
        take(kind, 0)
    load_gate.wait()
    load_up.wait()
    compute(FIRST, 0)
    for kind in range(2):
        take(kind, 1)
        take(kind, 3)
    for kind in range(2):
        take(kind, 2)
    compute(SECOND, 5)
    for step_f in range(RING):
        for kind in range(2):
            arrive(kind, step_f, 2)
            swap(kind, step_f, 2)
    compute(THIRD, 9)
    compute(FOURTH, 13)

    for step_p in range(RING):
        for step_z in range(RING):
            for relative in range(2):
                if (step_p, step_z, relative) != (0, 0, 0):
                    await_in(
                        landed.at[
                            (z + step_z) % RING, (p + step_p) % RING, (core + relative) % 2
                        ],
                        back_recv.at[2 * number_of(step_p, step_z) + relative],
                    )
    mine = pl.ds(pl.multiple_of(core * half_rows, half_rows), half_rows)
    blended = jnp.zeros((half_rows, actions_count), jnp.float32)
    for expert in range(RING):
        part_sum = jnp.zeros((half_rows, actions_count), jnp.float32)
        for place in range(RING):
            for which in range(2):
                part_sum = part_sum + landed[expert, place, which].astype(jnp.float32)
        blended = blended + share_buf[expert, mine, :] * part_sum
    halves[core] = blended
    send(
        halves.at[core], halves.at[core], pair_send.at[1], pair_recv.at[1], device(0, 0, other)
    )

    trace_row = trace_ref[...].astype(jnp.float32) / 1024.0
    trace_col = column(trace_row)
    reward_col = column(rewards_ref[...].astype(jnp.float32) * 0.25)
    action_col = column(actions_ref[...].astype(jnp.float32))
    log_row = jnp.log(DISCOUNT * trace_row)
    log_col = column(log_row)
    sums_row = jnp.sum(jnp.where(first_axis <= second_axis, log_col, 0.0), axis=0, keepdims=True)
    sums_col = jnp.sum(jnp.where(second_axis <= first_axis, log_row, 0.0), axis=1, keepdims=True)
    weight = jnp.where(
        first_axis >= second_axis, jnp.exp(jnp.minimum(sums_col - sums_row, 0.0)), 0.0
    )
    action_axis = lax.broadcasted_iota(jnp.int32, (rows, actions_count), 1).astype(jnp.float32)
    chosen = action_axis == action_col

    await_in(halves.at[other], pair_recv.at[1])
    values = jnp.concatenate([halves[0], halves[1]], axis=0)
    values_ref[...] = values
    greedy = jnp.max(values, axis=1, keepdims=True)
    taken = jnp.sum(jnp.where(chosen, values, 0.0), axis=1, keepdims=True)
    ahead_row = row_of(greedy - trace_col * taken)
    ahead = jnp.sum(
        jnp.where(second_axis == first_axis + 1, ahead_row, 0.0), axis=1, keepdims=True
    )
    driver = reward_col + DISCOUNT * ahead
    targets_ref[...] = jnp.sum(weight * driver, axis=0, keepdims=True)
    for copy in sends:
        copy.wait_send()


def per_device(
    tokens,
    norm_gain,
    expert_ids,
    gate_codes,
    gate_weights,
    up_weights,
    down_weights,
    value_head,
    actions,
    rewards,
    trace_codes,
):
    rows, wide = tokens.shape
    hidden_units, features = gate_weights.shape[1:]
    actions_count = value_head.shape[1]
    part = wide // 2
    held = (2, RING, RING, rows, part)
    most = max(len(group) for group in GROUPS) * rows
    vmem = pl.BlockSpec(memory_space=pltpu.VMEM)
    hbm = pl.BlockSpec(memory_space=pltpu.HBM)
    dma = pltpu.SemaphoreType.DMA
    blocks = RING * RING
    values, targets = pl.pallas_call(
        critic_kernel,
        out_shape=(
            jax.ShapeDtypeStruct((rows, actions_count), jnp.float32),
            jax.ShapeDtypeStruct((1, rows), jnp.float32),
        ),
        in_specs=[hbm, vmem, vmem, vmem, hbm, hbm, hbm, vmem, vmem, vmem, vmem],
        out_specs=(vmem, vmem),
        scratch_shapes=[
            pltpu.VMEM((2, rows, wide), jnp.bfloat16),
            pltpu.VMEM(held, jnp.bfloat16),
            pltpu.VMEM(held, jnp.bfloat16),
            pltpu.VMEM((hidden_units, features), jnp.bfloat16),
            pltpu.VMEM((hidden_units, features), jnp.bfloat16),
            pltpu.VMEM((hidden_units, features), jnp.bfloat16),
            pltpu.VMEM((hidden_units, 2 * actions_count), jnp.bfloat16),
            pltpu.VMEM((most, hidden_units), jnp.bfloat16),
            pltpu.VMEM((blocks, rows, actions_count), jnp.bfloat16),
            pltpu.VMEM((RING, RING, 2, rows // 2, actions_count), jnp.bfloat16),
            pltpu.VMEM((RING, rows, actions_count), jnp.float32),
            pltpu.VMEM((2, rows // 2, actions_count), jnp.float32),
            dma((4,)),
            dma((2,)),
            dma((2,)),
            dma((2, blocks + 1)),
            dma((2, blocks + 1)),
            dma((2, blocks)),
            dma((2, blocks)),
            dma((2 * blocks,)),
            dma((2 * blocks,)),
        ],
        compiler_params=pltpu.CompilerParams(
            collective_id=0, has_side_effects=True, vmem_limit_bytes=60 * 1024 * 1024
        ),
    )(
        tokens,
        norm_gain.reshape(1, -1),
        expert_ids.T,
        gate_codes.T,
        gate_weights,
        up_weights,
        down_weights,
        value_head,
        actions.reshape(1, -1),
        rewards.reshape(1, -1),
        trace_codes.reshape(1, -1),
    )
    return values, targets.reshape(-1)


def solution(mesh):
    in_specs = (
        P(("dp", "expert"), "tensor"),
        P(),
        P(("dp", "expert"), None),
        P(("dp", "expert"), None),
        P("expert", ("dp", "tensor"), None),
        P("expert", ("dp", "tensor"), None),
        P("expert", ("dp", "tensor"), None),
        P(),
        P(("dp", "expert")),
        P(("dp", "expert")),
        P(("dp", "expert")),
    )
    out_specs = (P(("dp", "expert"), None), P(("dp", "expert")))
    shape = mesh.shape
    rings = shape["dp"] == RING and shape["expert"] == RING and shape["tensor"] == 2
    body = per_device if rings else per_device_plain
    return jax.shard_map(
        body, mesh=mesh, in_specs=in_specs, out_specs=out_specs, check_vma=False
    )
```

time: 474 us -> 77.9 us (0.16)
  waiting for transfers between devices: 361 us -> 0 us
  Pallas kernels: 0 us -> 72.9 us
  matrix products: 48.9 us -> 0 us
  blocking collectives: 32 us -> 0 us
  between operations: 13.9 us -> 0.64 us
  other arithmetic: 9.03 us -> 0 us
  starting transfers between devices: 5.55 us -> 0 us
    reduce_scatter x1 -> x0, waiting for transfers between devices: 154 us -> none  [per_device(): lax.psum_scatter(expert_rows(gathered, gate_weights[0], up_weights[0], do...]
    all_gather x2 -> x0, waiting for transfers between devices: 98.3 us -> none  [the longest x1 88.6 us: per_device(): gathered = lax.all_gather(normed, 'dp', axis=0, tiled=True)]
    all_to_all x1 -> x0, waiting for transfers between devices: 92.9 us -> none  [per_device(): lax.all_to_all(payload.reshape(groups, capacity, payload.shape[1]), 'expe...]
    pallas_call x0 -> x1, Pallas kernels: none -> 72.9 us  [per_device(): pl.pallas_call(critic_kernel, out_shape=(jax.ShapeDtypeStruct((rows, acti...]
    dot_general x6 -> x0, matrix products: 48.9 us -> none  [the longest x1 26.7 us: expert_rows(): return jnp.dot(hidden, down_matrix, preferred_element_type=jnp.float32)]
    all_to_all x1 -> x0, blocking collectives: 32 us -> none  [per_device(): lax.all_to_all(outgoing, 'expert', split_axis=0, concat_axis=0, tiled=True)]
    psum x1 -> x0, waiting for transfers between devices: 15.5 us -> none  [per_device(): action_values = lax.psum(partial_values, 'tensor')]
    all_to_all x1 -> x0, starting transfers between devices: 4.99 us -> none  [per_device(): lax.all_to_all(payload.reshape(groups, capacity, payload.shape[1]), 'expe...]
  transfers between devices with their start and end apart: 5 -> 0, of which waited for: 5 -> 0; matrix products, arithmetic and copies ran while one was open for 0% -> 0% of each run, Pallas kernels for 0% -> 0%
where the time goes in v1:
time: 77.9 us; the launch traced here: 77.4 us
  Pallas kernels  72.9 us (94%)
  local copies, waits for them, and re-layouts  3.88 us (5%)
    pallas_call x1, Pallas kernels, per_device(): pl.pallas_call(critic_kernel, out_shape=(jax.ShapeDtypeStruct((rows, acti...  72.9 us
    unnamed x2, local copies, waits for them, and re-layouts  2.59 us

profile of v1, /device:TPU:0, one launch (start us, length us, event | category | flops | bytes accessed | tf_op | source)
XLA Modules:
  0.0 77.4 jit_solution(12891414236847224735)
XLA Ops:
  0.6 1.3 %reshape.19.gain_ref = bf16[1,2048]{1,0:T(2,128)(2,1)} reshape(bf16[2048]{0:T(1024)(128)(2,1)} %param.12) | data formatting | bytes 8192 | tf_op jit(solution)/shard_map/reshape | solution.py:518
  1.9 72.9 %shard_map.122 = (f32[128,128]{1,0:T(8,128)}, f32[1,128]{1,0:T(1,128)}) custom-call(bf16[128,1024]{1,0:T(8,128)(2,1)} %tokens_ref.1, bf16[1,2048]{1,0:T(2,128)(2,1)} %reshape.19.gain_ref, s32[2,128]{1,0:T(2,128)} %bitcast.6, s32[2,128]{1,0:T(2,128)} %bitcast.7, bf16[1,896,2048]{2,1,0:T(8,128)(2,1)} %gate_ref.1, bf16[1,896,2048]{2,1,0:T(8,128)(2,1)} %up_ref.1, ...), custom_call_target="tpu_custom_call" | custom-call | tf_op jit(solution)/shard_map/pallas_call | solution.py:482
  74.8 1.5 %copy.15 = f32[128,128]{1,0:T(8,128)} copy(f32[128,128]{1,0:T(8,128)} %get-tuple-element.8) | data formatting | bytes 131072
  76.3 1.1 %copy.16 = f32[128]{0:T(128)} copy(f32[128]{0:T(128)} %bitcast.11) | data formatting | bytes 1024

commit v2 on v1

--- a/solution.py
+++ b/solution.py
@@ -96,11 +96,7 @@
 RING = 4
 MESH = pl.DeviceIdType.MESH
 TILE = 128
-FIRST = ((0, 0), (1, 0), (3, 0), (0, 1), (0, 3))
-SECOND = ((1, 1), (1, 3), (3, 1), (3, 3))
-THIRD = ((2, 0), (0, 2), (2, 1), (1, 2))
-FOURTH = ((2, 3), (3, 2), (2, 2))
-GROUPS = (FIRST, SECOND, THIRD, FOURTH)
+ORDER = (0, 1, 3, 2)
 
 
 def gray(place):
@@ -129,6 +125,8 @@
     down_buf,
     scored_buf,
     hidden_buf,
+    partial,
+    given,
     sent,
     landed,
     share_buf,
@@ -138,8 +136,11 @@
     pair_recv,
     ring_send,
     ring_recv,
+    line_send,
     swap_send,
     swap_recv,
+    give_send,
+    give_recv,
     back_send,
     back_recv,
 ):
@@ -151,6 +152,7 @@
     rows = tokens_ref.shape[0]
     half_rows = rows // 2
     part = near.shape[-1]
+    planes = (z, z + 1 - 2 * (z % 2), jnp.where(z < 2, 2, 1), jnp.where(z < 2, 3, 0))
     wide = tokens_ref.shape[1]
     hidden_units = gate_ref.shape[1]
     actions_count = head_ref.shape[1]
@@ -170,29 +172,31 @@
     barrier = pltpu.get_barrier_semaphore()
     for step_p in range(RING):
         for step_z in range(RING):
-            for which in range(2):
-                if (step_p, step_z, which) != (0, 0, 0):
-                    pl.semaphore_signal(
-                        barrier,
-                        inc=1,
-                        device_id=device(step_p, step_z, (core + which) % 2),
-                        device_id_type=MESH,
-                    )
-    pl.semaphore_wait(barrier, 2 * RING * RING - 1)
+            if (step_p, step_z) != (0, 0):
+                pl.semaphore_signal(
+                    barrier, inc=1, device_id=device(step_p, step_z, core), device_id_type=MESH
+                )
+    pl.semaphore_signal(barrier, inc=1, device_id=device(0, 0, other), device_id_type=MESH)
+    pl.semaphore_wait(barrier, RING * RING)
 
     sends = []
 
-    def send(source, target, send_sem, recv_sem, to):
-        copy = pltpu.make_async_remote_copy(
-            src_ref=source,
-            dst_ref=target,
-            send_sem=send_sem,
-            recv_sem=recv_sem,
-            device_id=to,
-            device_id_type=MESH,
-        )
-        copy.start()
-        sends.append(copy)
+    def send(source, target, send_sem, recv_sem, to, condition=None):
+        def make():
+            return pltpu.make_async_remote_copy(
+                src_ref=source,
+                dst_ref=target,
+                send_sem=send_sem,
+                recv_sem=recv_sem,
+                device_id=to,
+                device_id_type=MESH,
+            )
+
+        if condition is None:
+            make().start()
+        else:
+            pl.when(condition)(lambda: make().start())
+        sends.append((condition, make))
 
     def await_in(target, recv_sem):
         pltpu.make_async_remote_copy(
@@ -236,49 +240,59 @@
             jnp.bfloat16
         )
         near[number, z, p] = normed[:, :part]
-        far[number, p, z] = normed[:, part:]
-
-    def block(kind, which, step_f, step_g):
-        if kind == 0:
-            return near.at[which, (z + step_g) % RING, (p + step_f) % RING]
-        return far.at[which, (p + step_g) % RING, (z + step_f) % RING]
-
-    def peer(kind, step_f, step_g):
-        if kind == 0:
-            return device(step_f, step_g, core)
-        return device(step_g, step_f, core)
-
-    def number_of(step_f, step_g):
-        return step_g * RING + step_f
-
+        far[number, z, p] = normed[:, part:]
+
+    buffers = (near, far)
     half = (pl.ds(0, half_rows), pl.ds(half_rows, half_rows))
-
-    def relay(kind, step_f, step_g, by_f, by_g, slot=None, cut=None):
-        source = block(kind, core, step_f, step_g)
-        seen = number_of((step_f - by_f) % RING, (step_g - by_g) % RING)
+    lower, upper = z > 0, z < RING - 1
+    inner = jnp.logical_and(lower, upper)
+
+    def block(kind, which, plane, step_f):
+        return buffers[kind].at[which, plane, (p + step_f) % RING]
+
+    def around(kind, plane, step_f, by, cut=None):
+        source = block(kind, core, plane, step_f)
+        seen = plane * 5 + (step_f - by) % RING
         if cut is not None:
             source = source.at[half[cut]]
-            seen = RING * RING if cut == 1 else seen
+            seen = plane * 5 + (4 if cut == 1 else 2)
         send(
             source,
             source,
             ring_send.at[kind, seen],
             ring_recv.at[kind, seen],
-            peer(kind, by_f, by_g),
+            device(by, 0, core),
         )
 
-    def arrive(kind, step_f, step_g):
-        here = block(kind, core, step_f, step_g)
-        seen = number_of(step_f, step_g)
-        if (step_f, step_g) == (2, 0):
-            await_in(here.at[half[0]], ring_recv.at[kind, seen])
-            await_in(here.at[half[1]], ring_recv.at[kind, RING * RING])
+    def along(kind, plane, step_f, to, condition, lane):
+        source = block(kind, core, plane, step_f)
+        send(
+            source,
+            source,
+            line_send.at[kind, lane, plane * RING + step_f],
+            ring_recv.at[kind, plane * 5 + step_f],
+            (dp, to, core),
+            condition,
+        )
+
+    def both_ways(kind, step_f):
+        along(kind, z, step_f, z + 1, upper, 0)
+        along(kind, z, step_f, z - 1, lower, 1)
+
+    def onward(kind, plane, step_f):
+        along(kind, plane, step_f, jnp.where(plane < z, z + 1, z - 1), inner, 0)
+
+    def arrive(kind, plane, step_f, split=False):
+        here = block(kind, core, plane, step_f)
+        if split:
+            await_in(here.at[half[0]], ring_recv.at[kind, plane * 5 + 2])
+            await_in(here.at[half[1]], ring_recv.at[kind, plane * 5 + 4])
         else:
-            await_in(here, ring_recv.at[kind, seen])
-
-    def swap(kind, step_f, step_g):
-        here = block(kind, core, step_f, step_g)
-        seen = number_of(step_f, step_g)
+            await_in(here, ring_recv.at[kind, plane * 5 + step_f])
+
+    def swap(kind, plane, step_f):
+        here = block(kind, core, plane, step_f)
+        seen = plane * RING + step_f
         send(
             here,
             here,
@@ -287,17 +301,40 @@
             device(0, 0, other),
         )
 
-    def swapped(kind, step_f, step_g):
-        await_in(
-            block(kind, other, step_f, step_g), swap_recv.at[kind, number_of(step_f, step_g)]
-        )
-
-    for kind in range(2):
-        relay(kind, 0, 0, 1, 0)
-        relay(kind, 0, 0, 3, 0)
-    for kind in range(2):
-        relay(kind, 0, 0, 0, 1)
-        relay(kind, 0, 0, 0, 3)
+    def swapped(kind, plane, step_f):
+        await_in(block(kind, other, plane, step_f), swap_recv.at[kind, plane * RING + step_f])
+
+    def turn(kind, plane):
+        for step_f in (1, 3):
+            arrive(kind, plane, step_f)
+            around(kind, plane, step_f, (4 - step_f) % RING, cut=0 if step_f == 3 else 1)
+        for step_f in (1, 3):
+            swap(kind, plane, step_f)
+
+    def turn_last(kind, plane):
+        arrive(kind, plane, 2, split=True)
+        swap(kind, plane, 2)
+
+    def passing(step, steps_f):
+        for step_f in steps_f:
+            arrive(0, planes[step], step_f)
+            onward(0, planes[step], step_f)
+            swap(0, planes[step], step_f)
+
+    def climb(step):
+        plane = planes[step]
+        arrive(1, plane, 0)
+        onward(1, plane, 0)
+        around(1, plane, 0, 1)
+        around(1, plane, 0, 3)
+        swap(1, plane, 0)
+
+    both_ways(1, 0)
+    around(0, z, 0, 1)
+    around(0, z, 0, 3)
+    both_ways(0, 0)
+    around(1, z, 0, 1)
+    around(1, z, 0, 3)
 
     load_down.wait()
     scored = jnp.dot(down_buf[...], head_ref[...], preferred_element_type=jnp.float32)
@@ -305,122 +342,144 @@
     scored_buf[:, :actions_count] = high
     scored_buf[:, actions_count:] = (scored - high.astype(jnp.float32)).astype(jnp.bfloat16)
 
-    for kind in range(2):
-        for step_f in (1, 3):
-            arrive(kind, step_f, 0)
-            relay(kind, step_f, 0, (4 - step_f) % RING, 0, cut=0 if step_f == 3 else 1)
-    for kind in range(2):
-        for step_f in (1, 3):
-            relay(kind, step_f, 0, 0, 1)
-            relay(kind, step_f, 0, 0, 3)
-            swap(kind, step_f, 0)
-    for kind in range(2):
-        arrive(kind, 2, 0)
-        relay(kind, 2, 0, 0, 1)
-        relay(kind, 2, 0, 0, 3)
-        swap(kind, 2, 0)
-
-    rising = (0, 1)
-
-    def take(kind, step_f):
-        for step_g in (1, 3):
-            arrive(kind, step_f, step_g)
-            if (step_g == 3) == (step_f in rising):
-                relay(kind, step_f, step_g, 0, (4 - step_g) % RING)
-            swap(kind, step_f, step_g)
-
-    def kinds(step_p, step_z):
-        return ((0, step_p, step_z), (1, step_z, step_p))
-
-    def compute(group, base):
-        for step_p, step_z in group:
-            if (step_p, step_z) != (0, 0):
-                for kind, step_f, step_g in kinds(step_p, step_z):
-                    swapped(kind, step_f, step_g)
-        lhs_rows = len(group) * rows
+    tiles = hidden_units // TILE
+    cuts = [tiles * number // 4 for number in range(5)]
+
+    def compute(step):
+        begin(step)
+        more(step, 1)
+        more(step, 2)
+        finish(step)
+
+    def begin(step):
+        plane = planes[step]
+        for step_f in ORDER:
+            if step > 0 or step_f > 0:
+                swapped(0, plane, step_f)
+                swapped(1, plane, step_f)
+        tile_span(plane, 0, cuts[1])
+
+    def more(step, number):
+        tile_span(planes[step], cuts[number], cuts[number + 1])
+
+    def tile_span(plane, first, last):
+        lhs_rows = RING * rows
 
         def tile(index, carry):
             at = pl.ds(pl.multiple_of(index * TILE, TILE), TILE)
             weights = jnp.concatenate([gate_buf[at, :], up_buf[at, :]], axis=0)
-            block_rows = []
-            for step_p, step_z in group:
-                zz, pp = (z + step_z) % RING, (p + step_p) % RING
-                block_rows.append(
-                    jnp.concatenate(
-                        [near[0, zz, pp], far[0, pp, zz], near[1, zz, pp], far[1, pp, zz]],
-                        axis=1,
-                    )
-                )
-            lhs = jnp.concatenate(block_rows, axis=0)
+            lhs = jnp.concatenate(
+                [
+                    buffer[which, plane].reshape(lhs_rows, buffer.shape[-1])
+                    for which in range(2)
+                    for buffer in buffers
+                ],
+                axis=1,
+            )
             both = lax.dot_general(
                 lhs, weights, (((1,), (1,)), ((), ())), preferred_element_type=jnp.float32
             )
-            hidden = (jax.nn.silu(both[:, :TILE]) * both[:, TILE:]).astype(jnp.bfloat16)
-            hidden_buf[:lhs_rows, at] = hidden
+            hidden_buf[:, at] = (jax.nn.silu(both[:, :TILE]) * both[:, TILE:]).astype(
+                jnp.bfloat16
+            )
             return carry
 
-        lax.fori_loop(0, hidden_units // TILE, tile, 0)
+        lax.fori_loop(first, last, tile, 0)
+
+    def finish(step):
+        tile_span(planes[step], cuts[3], tiles)
         result = jnp.dot(
-            hidden_buf[:lhs_rows, :], scored_buf[...], preferred_element_type=jnp.float32
+            hidden_buf[...], scored_buf[...], preferred_element_type=jnp.float32
         )
-        result = (result[:, :actions_count] + result[:, actions_count:]).astype(jnp.bfloat16)
-        for place, (step_p, step_z) in enumerate(group):
-            slot = base + place
-            sent[slot] = result[place * rows : (place + 1) * rows]
-            source = number_of((-step_p) % RING, (-step_z) % RING)
-            own = (step_p, step_z) == (0, 0)
-            if own:
-                landed[z, p, core] = sent[
-                    slot, pl.ds(pl.multiple_of(core * half_rows, half_rows), half_rows), :
-                ]
-                targets = ((other, 1),)
+        result = result[:, :actions_count] + result[:, actions_count:]
+        result = result.reshape(RING, 2, half_rows, actions_count)
+        partial[step, 0] = result[:, 0]
+        partial[step, 1] = result[:, 1]
+        send(
+            partial.at[step, other],
+            given.at[step],
+            give_send.at[step],
+            give_recv.at[step],
+            device(0, 0, other),
+        )
+
+    def give_back(step):
+        plane = planes[step]
+        await_in(given.at[step], give_recv.at[step])
+        sent[step] = (partial[step, core] + given[step]).astype(jnp.bfloat16)
+        for step_f in range(RING):
+            place = (p + step_f) % RING
+            if (step, step_f) == (0, 0):
+                landed[z, p] = sent[0, p]
             else:
-                targets = ((0, core % 2), (1, (core + 1) % 2))
-            for which, relative in targets:
-                cut = pl.ds(pl.multiple_of(which * half_rows, half_rows), half_rows)
                 send(
-                    sent.at[slot, cut],
-                    landed.at[z, p, core],
-                    back_send.at[2 * slot + which],
-                    back_recv.at[2 * source + relative],
-                    device(step_p, step_z, which),
+                    sent.at[step, place],
+                    landed.at[z, p],
+                    back_send.at[RING * step + step_f],
+                    back_recv.at[z * RING + (-step_f) % RING],
+                    (gray(place), plane, core),
                 )
 
-    for kind in range(2):
-        take(kind, 0)
+    turn(0, z)
+    both_ways(0, 1)
+    both_ways(0, 3)
+    climb(1)
+    arrive(0, z, 2, split=True)
+    both_ways(0, 2)
+    swap(0, z, 2)
+    turn(1, z)
+    passing(1, (0, 1, 3))
+    climb(2)
+    turn_last(1, z)
     load_gate.wait()
     load_up.wait()
-    compute(FIRST, 0)
-    for kind in range(2):
-        take(kind, 1)
-        take(kind, 3)
-    for kind in range(2):
-        take(kind, 2)
-    compute(SECOND, 5)
-    for step_f in range(RING):
-        for kind in range(2):
-            arrive(kind, step_f, 2)
-            swap(kind, step_f, 2)
-    compute(THIRD, 9)
-    compute(FOURTH, 13)
-
-    for step_p in range(RING):
-        for step_z in range(RING):
-            for relative in range(2):
-                if (step_p, step_z, relative) != (0, 0, 0):
-                    await_in(
-                        landed.at[
-                            (z + step_z) % RING, (p + step_p) % RING, (core + relative) % 2
-                        ],
-                        back_recv.at[2 * number_of(step_p, step_z) + relative],
-                    )
+    begin(0)
+    passing(1, (2,))
+    more(0, 1)
+    turn(1, planes[1])
+    more(0, 2)
+    passing(2, (0,))
+    climb(3)
+    finish(0)
+    passing(2, (1,))
+    turn_last(1, planes[1])
+    begin(1)
+    passing(2, (3,))
+    more(1, 1)
+    passing(2, (2,))
+    turn(1, planes[2])
+    more(1, 2)
+    give_back(0)
+    passing(3, (0,))
+    finish(1)
+    passing(3, (1,))
+    turn_last(1, planes[2])
+    begin(2)
+    passing(3, (3,))
+    more(2, 1)
+    turn(1, planes[3])
+    passing(3, (2,))
+    more(2, 2)
+    give_back(1)
+    finish(2)
+    turn_last(1, planes[3])
+    compute(3)
+    give_back(2)
+    give_back(3)
+
+    for step in range(RING):
+        for step_f in range(RING):
+            if (step, step_f) != (0, 0):
+                await_in(
+                    landed.at[planes[step], (p + step_f) % RING],
+                    back_recv.at[planes[step] * RING + step_f],
+                )
     mine = pl.ds(pl.multiple_of(core * half_rows, half_rows), half_rows)
     blended = jnp.zeros((half_rows, actions_count), jnp.float32)
     for expert in range(RING):
         part_sum = jnp.zeros((half_rows, actions_count), jnp.float32)
         for place in range(RING):
-            for which in range(2):
-                part_sum = part_sum + landed[expert, place, which].astype(jnp.float32)
+            part_sum = part_sum + landed[expert, place].astype(jnp.float32)
         blended = blended + share_buf[expert, mine, :] * part_sum
     halves[core] = blended
     send(
@@ -452,8 +511,11 @@
     )
     driver = reward_col + DISCOUNT * ahead
     targets_ref[...] = jnp.sum(weight * driver, axis=0, keepdims=True)
-    for copy in sends:
-        copy.wait_send()
+    for condition, make in sends:
+        if condition is None:
+            make().wait_send()
+        else:
+            pl.when(condition)(lambda make=make: make().wait_send())
 
 
 def per_device(
@@ -472,9 +534,9 @@
     rows, wide = tokens.shape
     hidden_units, features = gate_weights.shape[1:]
     actions_count = value_head.shape[1]
-    part = wide // 2
-    held = (2, RING, RING, rows, part)
-    most = max(len(group) for group in GROUPS) * rows
+    part = wide // 4
+    held = (2, RING, RING, rows)
+    half_rows = rows // 2
     vmem = pl.BlockSpec(memory_space=pltpu.VMEM)
     hbm = pl.BlockSpec(memory_space=pltpu.HBM)
     dma = pltpu.SemaphoreType.DMA
@@ -489,26 +551,31 @@
         out_specs=(vmem, vmem),
         scratch_shapes=[
             pltpu.VMEM((2, rows, wide), jnp.bfloat16),
-            pltpu.VMEM(held, jnp.bfloat16),
-            pltpu.VMEM(held, jnp.bfloat16),
+            pltpu.VMEM((*held, part), jnp.bfloat16),
+            pltpu.VMEM((*held, wide - part), jnp.bfloat16),
             pltpu.VMEM((hidden_units, features), jnp.bfloat16),
             pltpu.VMEM((hidden_units, features), jnp.bfloat16),
             pltpu.VMEM((hidden_units, features), jnp.bfloat16),
             pltpu.VMEM((hidden_units, 2 * actions_count), jnp.bfloat16),
-            pltpu.VMEM((most, hidden_units), jnp.bfloat16),
-            pltpu.VMEM((blocks, rows, actions_count), jnp.bfloat16),
-            pltpu.VMEM((RING, RING, 2, rows // 2, actions_count), jnp.bfloat16),
+            pltpu.VMEM((RING * rows, hidden_units), jnp.bfloat16),
+            pltpu.VMEM((RING, 2, RING, half_rows, actions_count), jnp.float32),
+            pltpu.VMEM((RING, RING, half_rows, actions_count), jnp.float32),
+            pltpu.VMEM((RING, RING, half_rows, actions_count), jnp.bfloat16),
+            pltpu.VMEM((RING, RING, half_rows, actions_count), jnp.bfloat16),
             pltpu.VMEM((RING, rows, actions_count), jnp.float32),
             pltpu.VMEM((2, rows // 2, actions_count), jnp.float32),
             dma((4,)),
             dma((2,)),
             dma((2,)),
-            dma((2, blocks + 1)),
-            dma((2, blocks + 1)),
+            dma((2, 5 * RING)),
+            dma((2, 5 * RING)),
+            dma((2, 2, blocks)),
             dma((2, blocks)),
             dma((2, blocks)),
-            dma((2 * blocks,)),
-            dma((2 * blocks,)),
+            dma((RING,)),
+            dma((RING,)),
+            dma((blocks,)),
+            dma((blocks,)),
         ],
         compiler_params=pltpu.CompilerParams(
             collective_id=0, has_side_effects=True, vmem_limit_bytes=60 * 1024 * 1024

time: 77.9 us -> 76.6 us (0.983)
  Pallas kernels: 72.9 us -> 71.6 us
    pallas_call x1, Pallas kernels: 72.9 us -> 71.6 us  [per_device(): pl.pallas_call(critic_kernel, out_shape=(jax.ShapeDtypeStruct((rows, acti...]
where the time goes in v2:
time: 76.6 us; the launch traced here: 76.2 us
  Pallas kernels  71.6 us (93%)
  local copies, waits for them, and re-layouts  3.88 us (5%)
    pallas_call x1, Pallas kernels, per_device(): pl.pallas_call(critic_kernel, out_shape=(jax.ShapeDtypeStruct((rows, acti...  71.6 us
    unnamed x2, local copies, waits for them, and re-layouts  2.59 us

profile of v2, /device:TPU:0, one launch (start us, length us, event | category | flops | bytes accessed | tf_op | source)
XLA Modules:
  0.0 76.2 jit_solution(17501294486678502851)
XLA Ops:
  0.6 1.3 %reshape.19.gain_ref = bf16[1,2048]{1,0:T(2,128)(2,1)} reshape(bf16[2048]{0:T(1024)(128)(2,1)} %param.12) | data formatting | bytes 8192 | tf_op jit(solution)/shard_map/reshape | solution.py:585
  1.9 71.6 %shard_map.122 = (f32[128,128]{1,0:T(8,128)}, f32[1,128]{1,0:T(1,128)}) custom-call(bf16[128,1024]{1,0:T(8,128)(2,1)} %tokens_ref.1, bf16[1,2048]{1,0:T(2,128)(2,1)} %reshape.19.gain_ref, s32[2,128]{1,0:T(2,128)} %bitcast.6, s32[2,128]{1,0:T(2,128)} %bitcast.7, bf16[1,896,2048]{2,1,0:T(8,128)(2,1)} %gate_ref.1, bf16[1,896,2048]{2,1,0:T(8,128)(2,1)} %up_ref.1, ...), custom_call_target="tpu_custom_call" | custom-call | tf_op jit(solution)/shard_map/pallas_call | solution.py:544
  73.6 1.5 %copy.15 = f32[128,128]{1,0:T(8,128)} copy(f32[128,128]{1,0:T(8,128)} %get-tuple-element.8) | data formatting | bytes 131072
  75.0 1.1 %copy.16 = f32[128]{0:T(128)} copy(f32[128]{0:T(128)} %bitcast.11) | data formatting | bytes 1024
